TPU v7x, 128 devices: a whole 4x4x4 slice. The times are simulated.
128 devices in a mesh: dp: 16 (over z, y), ep: 8 (over x, core).
Axes of the slice: x: 4, y: 4, z: 4, core: 2. Of those that a mesh axis runs over, the one named last changes fastest.
Arguments:
- x_in: bfloat16 [32768, 4096], P(('dp', 'ep'))
- ln_gain: float32 [4096], replicated
- ln_bias: float32 [4096], replicated
- w_router: bfloat16 [4096, 16], replicated
- w_gate: bfloat16 [16, 4096, 448], P('ep')
- w_up: bfloat16 [16, 4096, 448], P('ep')
- w_down: bfloat16 [16, 448, 4096], P('ep')
- expert_ids: int32 [32768, 2], P(('dp', 'ep'))
- slot_ids: int32 [32768, 2], P(('dp', 'ep'))
- d_out: bfloat16 [32768, 4096], P(('dp', 'ep'))
Outputs:
- output 1: bfloat16 [32768, 4096], P(('dp', 'ep'))
- output 2: bfloat16 [32768, 4096], P(('dp', 'ep'))
- output 3: float32 [4096], replicated
- output 4: float32 [4096], replicated
- output 5: float32 [4096, 16], replicated
- output 6: float32 [16, 4096, 448], P('ep')
- output 7: float32 [16, 4096, 448], P('ep')
- output 8: float32 [16, 448, 4096], P('ep')
All inputs are finite; a program needn't handle non-finite values.
Results may differ from a plain program's by a relative error of at most 0.00533895.
Values are sent between devices in bfloat16 or wider.
A program may use at most 1 GiB of HBM per device.

v0:
```python
import jax
import jax.numpy as jnp
from jax import lax
from jax.sharding import PartitionSpec as P

LN_EPS = 1e-5


def capacity_for(tokens_dev, experts, n_top):
    return 8 * ((5 * tokens_dev * n_top + 32 * experts - 1) // (32 * experts))


def norm_forward(x_loc, ln_gain, ln_bias):
    x_f = x_loc.astype(jnp.float32)
    mean_x = jnp.mean(x_f, axis=-1, keepdims=True)
    centered = x_f - mean_x
    var_x = jnp.mean(centered * centered, axis=-1, keepdims=True)
    inv_std = lax.rsqrt(var_x + LN_EPS)
    normed = centered * inv_std
    hidden = (normed * ln_gain + ln_bias).astype(jnp.bfloat16)
    return x_f, hidden, normed, inv_std


def norm_backward(d_hidden, normed, inv_std, ln_gain):
    d_normed = d_hidden * ln_gain
    mean_dn = jnp.mean(d_normed, axis=-1, keepdims=True)
    mean_dnn = jnp.mean(d_normed * normed, axis=-1, keepdims=True)
    return inv_std * (d_normed - mean_dn - normed * mean_dnn)


def router_forward(hidden, w_router, ids_loc):
    experts = w_router.shape[1]
    logits = jnp.dot(hidden, w_router, preferred_element_type=jnp.float32)
    pick_mask = (ids_loc[..., None] == jnp.arange(experts)).astype(jnp.float32)
    chosen = jnp.sum(pick_mask * logits[..., None, :], axis=-1)
    return jax.nn.softmax(chosen, axis=-1), pick_mask


def router_backward(gate_probs, pick_mask, pair_out, dout_f):
    d_gates = jnp.sum(pair_out * dout_f[:, None, :], axis=-1)
    d_chosen = gate_probs * (d_gates - jnp.sum(gate_probs * d_gates, axis=-1, keepdims=True))
    return jnp.sum(d_chosen[..., None] * pick_mask, axis=-2)


def expert_forward(expert_in, gate_loc, up_loc, down_loc):
    pre_gate = jnp.einsum("erm,emf->erf", expert_in, gate_loc, preferred_element_type=jnp.float32).astype(jnp.bfloat16)
    pre_up = jnp.einsum("erm,emf->erf", expert_in, up_loc, preferred_element_type=jnp.float32).astype(jnp.bfloat16)
    gate_f = pre_gate.astype(jnp.float32)
    act_mix = (gate_f * jax.nn.sigmoid(gate_f) * pre_up.astype(jnp.float32)).astype(jnp.bfloat16)
    expert_out = jnp.einsum("erf,efm->erm", act_mix, down_loc, preferred_element_type=jnp.float32).astype(jnp.bfloat16)
    return expert_out, (pre_gate, pre_up, act_mix)


def expert_backward(expert_in, saved, grad_in, gate_loc, up_loc, down_loc):
    pre_gate, pre_up, act_mix = saved
    d_mix = jnp.einsum("erm,efm->erf", grad_in, down_loc, preferred_element_type=jnp.float32).astype(jnp.bfloat16).astype(jnp.float32)
    grad_down = jnp.einsum("erf,erm->efm", act_mix, grad_in, preferred_element_type=jnp.float32)
    gate_f = pre_gate.astype(jnp.float32)
    sig_gate = jax.nn.sigmoid(gate_f)
    up_f = pre_up.astype(jnp.float32)
    d_pre_gate = (d_mix * up_f * sig_gate * (1.0 + gate_f * (1.0 - sig_gate))).astype(jnp.bfloat16)
    d_pre_up = (d_mix * gate_f * sig_gate).astype(jnp.bfloat16)
    grad_gate = jnp.einsum("erm,erf->emf", expert_in, d_pre_gate, preferred_element_type=jnp.float32)
    grad_up = jnp.einsum("erm,erf->emf", expert_in, d_pre_up, preferred_element_type=jnp.float32)
    d_expert_in = (jnp.einsum("erf,emf->erm", d_pre_gate, gate_loc, preferred_element_type=jnp.float32) + jnp.einsum("erf,emf->erm", d_pre_up, up_loc, preferred_element_type=jnp.float32)).astype(jnp.bfloat16)
    return d_expert_in, grad_gate, grad_up, grad_down


def solution(mesh):
    n_ep = mesh.shape["ep"]
    tok_spec = P(("dp", "ep"), None)
    exp_spec = P("ep", None, None)

    def local_step(x_loc, ln_gain, ln_bias, w_router, gate_loc, up_loc, down_loc, ids_loc, slots_loc, dout_loc):
        tokens_dev, model_dim = x_loc.shape
        experts = w_router.shape[1]
        local_exp = gate_loc.shape[0]
        n_top = ids_loc.shape[1]
        capacity = capacity_for(tokens_dev, experts, n_top)
        x_f, hidden, normed, inv_std = norm_forward(x_loc, ln_gain, ln_bias)
        gate_probs, pick_mask = router_forward(hidden, w_router, ids_loc)
        target = jnp.where(slots_loc >= 0, ids_loc * capacity + slots_loc, -1)
        pair_hot = (target[..., None] == jnp.arange(experts * capacity)).astype(jnp.bfloat16)
        token_hot = jnp.sum(pair_hot, axis=1)
        send_rows = jnp.einsum("ts,tm->sm", token_hot, hidden, preferred_element_type=jnp.float32).astype(jnp.bfloat16)
        expert_in = lax.all_to_all(send_rows.reshape(n_ep, local_exp, capacity, model_dim), "ep", 0, 2, tiled=True)
        expert_in = expert_in.reshape(local_exp, n_ep * capacity, model_dim)
        expert_out, saved = expert_forward(expert_in, gate_loc, up_loc, down_loc)
        ret_rows = lax.all_to_all(expert_out.reshape(1, local_exp, n_ep * capacity, model_dim), "ep", 2, 0, tiled=True)
        ret_rows = ret_rows.reshape(experts * capacity, model_dim)
        pair_out = jnp.dot(pair_hot.reshape(tokens_dev * n_top, experts * capacity), ret_rows, preferred_element_type=jnp.float32).reshape(tokens_dev, n_top, model_dim)
        mixed = jnp.sum(gate_probs[..., None] * pair_out, axis=1)
        moe_out = (x_f + mixed).astype(jnp.bfloat16)
        dout_f = dout_loc.astype(jnp.float32)
        d_logits = router_backward(gate_probs, pick_mask, pair_out, dout_f)
        pair_grad = (gate_probs[..., None] * dout_f[:, None, :]).astype(jnp.bfloat16)
        send_grad = jnp.einsum("tks,tkm->sm", pair_hot, pair_grad, preferred_element_type=jnp.float32).astype(jnp.bfloat16)
        grad_in = lax.all_to_all(send_grad.reshape(n_ep, local_exp, capacity, model_dim), "ep", 0, 2, tiled=True)
        grad_in = grad_in.reshape(local_exp, n_ep * capacity, model_dim)
        d_expert_in, grad_gate, grad_up, grad_down = expert_backward(expert_in, saved, grad_in, gate_loc, up_loc, down_loc)
        d_rows = lax.all_to_all(d_expert_in.reshape(1, local_exp, n_ep * capacity, model_dim), "ep", 2, 0, tiled=True)
        d_rows = d_rows.reshape(experts * capacity, model_dim)
        d_hidden_moe = jnp.einsum("ts,sm->tm", token_hot, d_rows, preferred_element_type=jnp.float32)
        d_hidden_router = jnp.einsum("te,me->tm", d_logits, w_router, preferred_element_type=jnp.float32)
        d_hidden = (d_hidden_moe + d_hidden_router).astype(jnp.bfloat16).astype(jnp.float32)
        grad_x = (dout_f + norm_backward(d_hidden, normed, inv_std, ln_gain)).astype(jnp.bfloat16)
        small_sums = lax.psum((jnp.sum(d_hidden * normed, axis=0), jnp.sum(d_hidden, axis=0), jnp.einsum("tm,te->me", hidden, d_logits, preferred_element_type=jnp.float32)), ("dp", "ep"))
        expert_sums = lax.psum((grad_gate, grad_up, grad_down), "dp")
        return (moe_out, grad_x) + tuple(small_sums) + tuple(expert_sums)

    return jax.shard_map(local_step, mesh=mesh, in_specs=(tok_spec, P(None), P(None), P(None, None), exp_spec, exp_spec, exp_spec, tok_spec, tok_spec, tok_spec), out_specs=(tok_spec, tok_spec, P(None), P(None), P(None, None), exp_spec, exp_spec, exp_spec), check_vma=False)
```

profile of v0, /device:TPU:1, one launch (start us, length us, event | category | flops | bytes accessed | tf_op | source)
XLA Modules:
  0.0 922.3 jit_solution(14182160179800947)
XLA Ops:
  7.2 0.0 copy-start
  7.2 0.0 copy-start.2
  7.2 0.0 copy-start.13
  7.2 0.0 copy-start.21
  7.2 0.0 copy-start.11
  7.2 2.1 convert_reduce_fusion.1
  9.3 0.0 copy-start.15
  9.4 2.3 fusion.16
  11.7 0.0 copy-start.19
  11.7 0.3 fusion.36
  12.0 0.3 copy-done.17
  12.3 1.0 fusion.11
  13.3 0.0 copy-start.3
  13.3 3.9 convolution_convert_fusion
  17.2 5.9 all-to-all-start
  23.1 4.2 convert_element_type.82
  27.3 0.6 fusion.51
  28.1 0.0 copy-start.22
  28.1 6.3 bitcast_convert_fusion
  34.4 48.5 %all-to-all-done = bf16[8,2,40,4096]{3,2,1,0:T(8,128)(2,1)} async-done(((bf16[8,2,40,4096]{3,2,1,0:T(8,128)(2,1)}), bf16[8,2,40,4096]{3,2,1,0:T(8,128)(2,1)}, u32[]{:S(2)}, u32[]{:S(2)}) %all-to-all-start) | async-done | bytes 5242912 | tf_op jit(solution)/shard_map/all_to_all | solution.py:86
  82.9 5.9 all-to-all-start.2
  88.8 0.0 slice-start.2
  88.8 3.0 copy.49
  91.8 0.0 slice-start.3
  91.8 7.9 convolution_convert_fusion.4
  99.8 2.9 convolution_convert_fusion.3
  102.7 0.0 copy-start.9
  102.7 0.8 copy-done.9
  103.5 8.0 fusion.3
  111.6 10.2 %copy.50 = bf16[1,2,320,4096]{3,1,0,2:T(2,128)(2,1)} copy(bf16[1,2,320,4096]{3,2,1,0:T(8,128)(2,1)} %fusion.3) | data formatting | bytes 10485760 | tf_op jit(solution)/shard_map/reshape | solution.py:89
  121.8 26.8 %all-to-all-done.2 = bf16[8,2,40,4096]{3,2,1,0:T(8,128)(2,1)} async-done(((bf16[8,2,40,4096]{3,2,1,0:T(8,128)(2,1)}), bf16[8,2,40,4096]{3,2,1,0:T(8,128)(2,1)}, u32[]{:S(2)}, u32[]{:S(2)}) %all-to-all-start.2) | async-done | bytes 5242912 | tf_op jit(solution)/shard_map/all_to_all | solution.py:98
  148.6 5.6 all-to-all-start.1
  154.2 2.8 copy.52
  157.0 0.0 copy-start.10
  157.1 0.0 slice-start
  157.1 6.3 convolution_convert_fusion.2
  163.4 0.0 slice-start.1
  163.4 8.1 fusion.44
  171.5 7.7 fusion.47
  179.2 34.8 %all-to-all-done.1 = bf16[1,2,320,4096]{3,1,0,2:T(2,128)(2,1)} async-done(((bf16[1,2,320,4096]{3,1,0,2:T(2,128)(2,1)}), bf16[1,2,320,4096]{3,1,0,2:T(2,128)(2,1)}, u32[]{:S(2)}, u32[]{:S(2)}) %all-to-all-start.1) | async-done | bytes 5242912 | tf_op jit(solution)/shard_map/all_to_all | solution.py:89
  214.0 6.4 copy.51
  220.5 0.0 copy-start.5
  220.5 6.7 multiply_reduce_fusion
  227.3 1.1 fusion.53
  228.4 0.0 all-reduce.5.cloned.1.call-update
  228.4 0.2 all-reduce.7.cloned.1.call-start
  228.6 12.1 %fusion.41 = f32[2,4096,448]{1,2,0:T(8,128)} fusion(bf16[2,320,4096]{2,1,0:T(8,128)(2,1)} %bitcast.56, bf16[2,320,448]{2,1,0:T(8,128)(2,1)S(1)} %convolution_convert_fusion.4, bf16[2,320,448]{2,1,0:T(8,128)(2,1)S(1)} %convolution_convert_fusion.2), kind=kOutput, calls=%fused_computation.76 | convolution fusion | flops 2351104000 | bytes 21069824 | tf_op jit(solution)/shard_map/erm,erf->emf/dot_general | solution.py:64
  240.7 0.0 all-reduce.7.cloned.1.call-update
  240.7 5.9 fusion.49
  246.6 8.2 fusion.4
  254.8 10.3 %copy.53 = bf16[1,2,320,4096]{3,1,0,2:T(2,128)(2,1)} copy(bf16[1,2,320,4096]{3,2,1,0:T(8,128)(2,1)} %fusion.4) | data formatting | bytes 10485760 | tf_op jit(solution)/shard_map/reshape | solution.py:101
  265.1 65.2 %all_to_all.60 = bf16[1,2,320,4096]{3,1,0,2:T(2,128)(2,1)S(1)} all-to-all(bf16[1,2,320,4096]{3,1,0,2:T(2,128)(2,1)} %copy.53), channel_id=1, replica_groups=mesh['dp'=16,'ep'=8] {'ep'}, dimensions={2} | all-to-all | bytes 10485760 | tf_op jit(solution)/shard_map/all_to_all | solution.py:101
  330.3 3.7 copy.54
  334.0 0.6 copy.55
  334.7 0.3 copy-done.7
  335.0 1.8 fusion.52
  336.8 3.1 fusion.19
  340.0 67.8 %all-reduce = (f32[4096]{0:T(1024)}, f32[4096]{0:T(1024)}) all-reduce(f32[4096]{0:T(1024)S(1)} %get-tuple-element.10, f32[4096]{0:T(1024)S(1)} %get-tuple-element.13), channel_id=1, replica_groups=mesh['dp'=16,'ep'=8] {'dp','ep'}, use_global_device_ids=true, to_apply=%region_13.14 | all-reduce | flops 8192 | bytes 65536 | tf_op jit(solution)/shard_map/psum | solution.py:107
  407.8 6.0 fusion.15
  413.8 462.3 %all-reduce.7.cloned.1.call-done = (f32[2,4096,448]{1,2,0:T(8,128)}, f32[2,4096,448]{1,2,0:T(8,128)}, f32[2,448,4096]{2,1,0:T(8,128)}) async-done(((f32[2,4096,448]{1,2,0:T(8,128)}, f32[2,4096,448]{1,2,0:T(8,128)}, f32[2,448,4096]{2,1,0:T(8,128)}), (f32[2,4096,448]{1,2,0:T(8,128)}, f32[2,4096,448]{1,2,0:T(8,128)}, f32[2,448,4096]{2,1,0:T(8,128)})) %all-reduce.7.cloned.1.call-update) | async-done | bytes 44040208 | tf_op jit(solution)/shard_map/psum | solution.py:108
  876.1 1.7 copy.60
  877.7 12.5 %copy.61 = f32[2,4096,448]{1,2,0:T(8,128)} copy(f32[2,4096,448]{1,2,0:T(8,128)} %get-tuple-element.29) | data formatting | bytes 29360128
  890.2 12.5 %copy.62 = f32[2,4096,448]{1,2,0:T(8,128)} copy(f32[2,4096,448]{1,2,0:T(8,128)} %get-tuple-element.30) | data formatting | bytes 29360128
  902.7 12.5 %copy.63 = f32[2,448,4096]{2,1,0:T(8,128)} copy(f32[2,448,4096]{2,1,0:T(8,128)} %get-tuple-element.31) | data formatting | bytes 29360128
  (52 shorter events, 0.2 us)
Async XLA Ops:
  7.2 20.1 %copy-start = (bf16[4096,16]{0,1:T(8,128)(2,1)S(1)}, bf16[4096,16]{0,1:T(8,128)(2,1)}, u32[]{:S(2)}) copy-start(bf16[4096,16]{0,1:T(8,128)(2,1)} %param.13) | copy-start | bytes 393220
  7.2 5.1 copy-start.2
  7.2 4.5 copy-start.13
  7.2 4.5 copy-start.21
  7.2 5.0 copy-start.11
  7.2 5.0 copy-start.14
  9.3 2.6 copy-start.15
  11.7 0.6 copy-start.17
  11.7 16.4 %copy-start.19 = (s32[256,2]{0,1:T(2,128)}, s32[256,2]{0,1:T(2,128)S(1)}, u32[]{:S(2)}) copy-start(s32[256,2]{0,1:T(2,128)S(1)} %compare_select_fusion) | copy-start | bytes 6148
  12.3 4.9 copy-start.6
  13.3 3.9 copy-start.3
  17.2 65.7 %all-to-all-start = ((bf16[8,2,40,4096]{3,2,1,0:T(8,128)(2,1)}), bf16[8,2,40,4096]{3,2,1,0:T(8,128)(2,1)}, u32[]{:S(2)}, u32[]{:S(2)}) async-start(bf16[8,2,40,4096]{3,2,1,0:T(8,128)(2,1)} %bitcast.61), calls=%async_computation | async-start | bytes 10485760 | tf_op jit(solution)/shard_map/all_to_all | solution.py:86
  23.1 4.2 copy-start.4
  28.1 6.4 copy-start.22
  82.9 65.6 %all-to-all-start.2 = ((bf16[8,2,40,4096]{3,2,1,0:T(8,128)(2,1)}), bf16[8,2,40,4096]{3,2,1,0:T(8,128)(2,1)}, u32[]{:S(2)}, u32[]{:S(2)}) async-start(bf16[8,2,40,4096]{3,2,1,0:T(8,128)(2,1)} %bitcast.67), calls=%async_computation.2 | async-start | bytes 10485760 | tf_op jit(solution)/shard_map/all_to_all | solution.py:98
  88.8 11.0 %slice-start.2 = ((s8[7340032]{0:T(1024)(128)(4,1)}), s8[4194304]{0:T(1024)(128)(4,1)S(1)}, s32[]{:S(2)}) async-start(s8[7340032]{0:T(1024)(128)(4,1)} %bitcast.65), calls=%async_computation.8 | async-start | bytes 8388608
  91.8 7.9 copy-start.1
  91.8 8.0 slice-start.3
  102.7 0.8 copy-start.9
  148.6 65.5 %all-to-all-start.1 = ((bf16[1,2,320,4096]{3,1,0,2:T(2,128)(2,1)}), bf16[1,2,320,4096]{3,1,0,2:T(2,128)(2,1)}, u32[]{:S(2)}, u32[]{:S(2)}) async-start(bf16[1,2,320,4096]{3,1,0,2:T(2,128)(2,1)} %copy.50), calls=%async_computation.1 | async-start | bytes 10485760 | tf_op jit(solution)/shard_map/all_to_all | solution.py:89
  154.2 259.6 %all-reduce.5.cloned.1.call-start = ((), (), s32[]{:S(2)}) async-start(), calls=%async_computation.4 | async-start | bytes 524288 | tf_op jit(solution)/shard_map/psum | solution.py:107
  157.0 6.3 copy-start.10
  157.1 14.4 %slice-start = ((s8[5242880]{0:T(1024)(128)(4,1)}), s8[4194304]{0:T(1024)(128)(4,1)S(1)}, s32[]{:S(2)}) async-start(s8[5242880]{0:T(1024)(128)(4,1)} %bitcast.57), calls=%async_computation.6 | async-start | bytes 8388608
  163.4 8.1 slice-start.1
  214.0 6.4 copy-start.8
  214.0 6.4 copy-start.20
  214.0 6.4 copy-start.23
  220.5 6.8 copy-start.5
  228.4 647.7 %all-reduce.7.cloned.1.call-start = ((), (), s32[]{:S(2)}) async-start(), calls=%async_computation.5 | async-start | bytes 88080384 | tf_op jit(solution)/shard_map/psum | solution.py:108
  334.0 1.0 copy-start.7
  335.0 1.8 copy-start.12
  335.0 1.8 copy-start.16
  335.0 1.9 copy-start.18
Sparse Core Ops, SparseCore 0:
  228.5 149.5 all-reduce.4
  383.2 492.8 all-reduce.6
where the time goes:
time: 928 us; the launch traced here: 922 us
  waiting for transfers between devices  572 us (62%)
  blocking collectives  133 us (14%)
  matrix products  90.7 us (10%)
  local copies, waits for them, and re-layouts  77.8 us (8%)
  starting transfers between devices  17.6 us (2%)
  other arithmetic  16 us (2%)
  between operations  14.7 us (2%)
    psum x1, waiting for transfers between devices, local_step(): expert_sums = lax.psum((grad_gate, grad_up, grad_down), 'dp')  462 us
    psum x1, blocking collectives, local_step(): lax.psum((jnp.sum(d_hidden * normed, axis=0), jnp.sum(d_hidden, axis=0),...  67.8 us
    all_to_all x1, blocking collectives, local_step(): lax.all_to_all(d_expert_in.reshape(1, local_exp, n_ep * capacity, model_d...  65.2 us
    all_to_all x1, waiting for transfers between devices, local_step(): lax.all_to_all(send_rows.reshape(n_ep, local_exp, capacity, model_dim), '...  48.5 us
    unnamed x60, local copies, waits for them, and re-layouts  40.7 us
    all_to_all x1, waiting for transfers between devices, local_step(): lax.all_to_all(expert_out.reshape(1, local_exp, n_ep * capacity, model_di...  34.8 us
    all_to_all x1, waiting for transfers between devices, local_step(): lax.all_to_all(send_grad.reshape(n_ep, local_exp, capacity, model_dim), '...  26.8 us
  transfers between devices with their start and end apart: 5, of which 4 were waited for; matrix products, arithmetic and copies ran while one was open for 13% of the time, Pallas kernels for 0%

commit v1 on v0

v1 whole, which is shorter than its diff:
```python
import jax
import jax.numpy as jnp
from jax import lax
from jax.experimental import pallas as pl
from jax.sharding import Mesh, PartitionSpec as P

LN_EPS = 1e-5
BF = jnp.bfloat16
F32 = jnp.float32
NZ = NY = NX = 4
NC = 2
AXES = ("z", "y", "x", "c")


def capacity_for(tokens_dev, experts, n_top):
    return 8 * ((5 * tokens_dev * n_top + 32 * experts - 1) // (32 * experts))


def norm_forward(x_loc, ln_gain, ln_bias):
    x_f = x_loc.astype(F32)
    mean_x = jnp.mean(x_f, axis=-1, keepdims=True)
    centered = x_f - mean_x
    var_x = jnp.mean(centered * centered, axis=-1, keepdims=True)
    inv_std = lax.rsqrt(var_x + LN_EPS)
    normed = centered * inv_std
    hidden = (normed * ln_gain + ln_bias).astype(BF)
    return x_f, hidden, normed, inv_std


def norm_backward(d_hidden, normed, inv_std, ln_gain):
    d_normed = d_hidden * ln_gain
    mean_dn = jnp.mean(d_normed, axis=-1, keepdims=True)
    mean_dnn = jnp.mean(d_normed * normed, axis=-1, keepdims=True)
    return inv_std * (d_normed - mean_dn - normed * mean_dnn)


def router_forward(hidden, w_router, ids_loc):
    experts = w_router.shape[1]
    logits = jnp.dot(hidden, w_router, preferred_element_type=F32)
    pick_mask = (ids_loc[..., None] == jnp.arange(experts)).astype(F32)
    chosen = jnp.sum(pick_mask * logits[..., None, :], axis=-1)
    return jax.nn.softmax(chosen, axis=-1), pick_mask


def router_backward(gate_probs, pick_mask, pair_out, dout_f):
    d_gates = jnp.sum(pair_out * dout_f[:, None, :], axis=-1)
    d_chosen = gate_probs * (d_gates - jnp.sum(gate_probs * d_gates, axis=-1, keepdims=True))
    return jnp.sum(d_chosen[..., None] * pick_mask, axis=-2)


def home_of(expert):
    x, local = expert // 4, expert % 4
    y = (local >> 1) | ((local & 1) << 1)
    return y * NX + x


def weights_here(w_loc):
    y, c = lax.axis_index("y"), lax.axis_index("c")
    mine = lax.dynamic_index_in_dim(w_loc, y >> 1, 0, keepdims=False)
    pairs = [(yy * NC + (yy & 1), yy * NC + 1 - (yy & 1)) for yy in range(NY)]
    other = lax.ppermute(mine, ("y", "c"), pairs)
    return jnp.where(c == (y & 1), mine, other)


def to_owner_core(grad):
    pairs = []
    for yy in range(NY):
        own = yy & 1
        pairs.append((yy * NC + own, yy * NC + own))
        pairs.append((yy * NC + 1 - own, (yy ^ 1) * NC + own))
    return lax.ppermute(grad, ("y", "c"), pairs)


def dispatch(rows):
    return lax.all_to_all(rows, ("y", "x"), 0, 0, tiled=True)


def reduce_grad(factor_pair, rows):
    c = lax.axis_index("c")
    first, second = factor_pair
    away = jnp.where(c == 0, second, first)
    here = jnp.where(c == 0, first, second)
    partial = jnp.einsum("rf,rm->fm", away, rows, preferred_element_type=F32)
    sent = lax.ppermute(partial, "c", [(0, 1), (1, 0)])
    pair = jnp.einsum("rf,rm->fm", here, rows, preferred_element_type=F32) + sent
    return lax.psum_scatter(pair, "z", scatter_dimension=0, tiled=True)


def copy_out(array):
    n, rows, d = array.shape
    step = rows // 4

    def body(src_ref, dst_ref):
        dst_ref[...] = src_ref[...]

    return pl.pallas_call(
        body,
        grid=(n, 4),
        in_specs=[pl.BlockSpec((1, step, d), lambda i, k: (i, k, 0))],
        out_specs=pl.BlockSpec((1, step, d), lambda i, k: (i, k, 0)),
        out_shape=jax.ShapeDtypeStruct(array.shape, array.dtype),
        cost_estimate=pl.CostEstimate(flops=5000000000, bytes_accessed=8 * n * rows * d, transcendentals=0),
    )(array)


def gather_grad(grad):
    full = lax.all_gather(grad, ("y", "z"), axis=0, tiled=True)
    return full.reshape(2, full.shape[0] // 2, full.shape[1])


def small_psum(parts):
    stacked = jnp.concatenate(parts, axis=0)
    rows, d = stacked.shape
    n = NX * NC
    cut = jnp.swapaxes(stacked.reshape(rows, n, d // n), 0, 1)
    got = lax.all_to_all(cut, ("x", "c"), 0, 0, tiled=True)
    part = jnp.sum(got, axis=0)
    part = jnp.sum(lax.all_gather(part, ("z", "y"), axis=0, tiled=False), axis=0)
    full = lax.all_gather(part, ("x", "c"), axis=0, tiled=False)
    return jnp.swapaxes(full, 0, 1).reshape(rows, d)


def solution(mesh):
    inner = Mesh(mesh.devices.reshape(NZ, NY, NX, NC), AXES)
    tok_spec = P(AXES, None)
    exp_spec = P(("x", "c"), None, None)

    def local_step(x_loc, ln_gain, ln_bias, w_router, gate_loc, up_loc, down_loc, ids_loc, slots_loc, dout_loc):
        tokens_dev, model_dim = x_loc.shape
        experts = w_router.shape[1]
        n_top = ids_loc.shape[1]
        capacity = capacity_for(tokens_dev, experts, n_top)
        slots = experts * capacity
        w_gate = weights_here(gate_loc)
        w_up = weights_here(up_loc)
        w_down = weights_here(down_loc)
        x_f, hidden, normed, inv_std = norm_forward(x_loc, ln_gain, ln_bias)
        gate_probs, pick_mask = router_forward(hidden, w_router, ids_loc)
        target = jnp.where(slots_loc >= 0, home_of(ids_loc) * capacity + slots_loc, -1)
        pair_hot = (target[..., None] == jnp.arange(slots)).astype(BF)
        token_hot = jnp.sum(pair_hot, axis=1)
        send_rows = jnp.einsum("ts,tm->sm", token_hot, hidden, preferred_element_type=F32).astype(BF)
        expert_in = dispatch(send_rows)
        send_rows, dout_late = lax.optimization_barrier((send_rows, dout_loc))
        dout_f = dout_late.astype(F32)
        pair_grad = (gate_probs[..., None] * dout_f[:, None, :]).astype(BF)
        send_grad = jnp.einsum("tks,tkm->sm", pair_hot, pair_grad, preferred_element_type=F32).astype(BF)
        grad_in = dispatch(send_grad)

        pre_gate = jnp.dot(expert_in, w_gate, preferred_element_type=F32).astype(BF)
        pre_up = jnp.dot(expert_in, w_up, preferred_element_type=F32).astype(BF)
        gate_f = pre_gate.astype(F32)
        up_f = pre_up.astype(F32)
        sig_gate = jax.nn.sigmoid(gate_f)
        act_mix = (gate_f * sig_gate * up_f).astype(BF)
        expert_out = jnp.dot(act_mix, w_down, preferred_element_type=F32).astype(BF)

        expert_out, grad_in = lax.optimization_barrier((expert_out, grad_in))
        d_mix = jnp.einsum("rm,fm->rf", grad_in, w_down, preferred_element_type=F32).astype(BF).astype(F32)
        d_pre_gate = (d_mix * up_f * sig_gate * (1.0 + gate_f * (1.0 - sig_gate))).astype(BF)
        d_pre_up = (d_mix * gate_f * sig_gate).astype(BF)

        ff = act_mix.shape[1]
        ret_rows = dispatch(expert_out)
        grad_down = reduce_grad((act_mix[:, : ff // 2], act_mix[:, ff // 2 :]), grad_in)
        grad_gate_up = reduce_grad((d_pre_gate, d_pre_up), expert_in)
        d_expert_in = (jnp.einsum("rf,mf->rm", d_pre_gate, w_gate, preferred_element_type=F32) + jnp.einsum("rf,mf->rm", d_pre_up, w_up, preferred_element_type=F32)).astype(BF)
        ret_rows, d_expert_in = lax.optimization_barrier((ret_rows, d_expert_in))
        d_rows = dispatch(d_expert_in)
        grad_down = to_owner_core(grad_down)
        grad_down, grad_gate_up, d_rows = lax.optimization_barrier((grad_down, grad_gate_up, d_rows))
        full_down = copy_out(gather_grad(grad_down))
        gate_up = gather_grad(to_owner_core(grad_gate_up))
        full_gate = jnp.swapaxes(gate_up[:, :ff], 1, 2)
        full_up = jnp.swapaxes(gate_up[:, ff:], 1, 2)

        pair_out = jnp.dot(pair_hot.reshape(tokens_dev * n_top, slots), ret_rows, preferred_element_type=F32).reshape(tokens_dev, n_top, model_dim)
        mixed = jnp.sum(gate_probs[..., None] * pair_out, axis=1)
        moe_out = (x_f + mixed).astype(BF)
        d_logits = router_backward(gate_probs, pick_mask, pair_out, dout_f)
        d_hidden_moe = jnp.einsum("ts,sm->tm", token_hot, d_rows, preferred_element_type=F32)
        d_hidden_router = jnp.einsum("te,me->tm", d_logits, w_router, preferred_element_type=F32)
        d_hidden = (d_hidden_moe + d_hidden_router).astype(BF).astype(F32)
        grad_x = (dout_f + norm_backward(d_hidden, normed, inv_std, ln_gain)).astype(BF)
        small = small_psum([jnp.einsum("te,tm->em", d_logits, hidden, preferred_element_type=F32), jnp.sum(d_hidden * normed, axis=0)[None], jnp.sum(d_hidden, axis=0)[None]])
        return (moe_out, grad_x, small[experts], small[experts + 1], small[:experts].T, full_gate, full_up, full_down)

    return jax.shard_map(local_step, mesh=inner, in_specs=(tok_spec, P(None), P(None), P(None, None), exp_spec, exp_spec, exp_spec, tok_spec, tok_spec, tok_spec), out_specs=(tok_spec, tok_spec, P(None), P(None), P(None, None), exp_spec, exp_spec, exp_spec), check_vma=False)
```

time: 928 us -> 719 us (0.77)
  waiting for transfers between devices: 572 us -> 440 us
  blocking collectives: 133 us -> 43 us
  local copies, waits for them, and re-layouts: 77.8 us -> 38.1 us
  starting transfers between devices: 17.6 us -> 42 us
  Pallas kernels: 0 us -> 13.1 us
  matrix products: 90.7 us -> 102 us
    psum x2 -> x0, waiting for transfers between devices: 462 us -> none  [the longest x1 462 us: local_step(): expert_sums = lax.psum((grad_gate, grad_up, grad_down), 'dp')]
    all_gather x0 -> x2, waiting for transfers between devices: none -> 154 us  [gather_grad(): full = lax.all_gather(grad, ('y', 'z'), axis=0, tiled=True)]
    all_to_all x3 -> x5, waiting for transfers between devices: 110 us -> 244 us  [the longest x4 243 us: dispatch(): return lax.all_to_all(rows, ('y', 'x'), 0, 0, tiled=True)]
    psum x1 -> x0, blocking collectives: 67.8 us -> none  [local_step(): lax.psum((jnp.sum(d_hidden * normed, axis=0), jnp.sum(d_hidden, axis=0),...]
    all_to_all x1 -> x0, blocking collectives: 65.2 us -> none  [local_step(): lax.all_to_all(d_expert_in.reshape(1, local_exp, n_ep * capacity, model_d...]
    all_gather x0 -> x2, blocking collectives: none -> 43 us  [the longest x1 25.9 us: small_psum(): lax.all_gather(part, ('z', 'y'), axis=0, tiled=False)]
    ppermute x0 -> x7, waiting for transfers between devices: none -> 41.9 us  [the longest x2 36 us: to_owner_core(): return lax.ppermute(grad, ('y', 'c'), pairs)]
    unnamed x60 -> x73, local copies, waits for them, and re-layouts: 40.7 us -> 1.11 us
  transfers between devices with their start and end apart: 5 -> 16, of which waited for: 4 -> 8; matrix products, arithmetic and copies ran while one was open for 13% -> 17% of each run, Pallas kernels for 0% -> 2%
where the time goes in v1:
time: 719 us; the launch traced here: 710 us
  waiting for transfers between devices  440 us (61%)
  matrix products  102 us (14%)
  blocking collectives  43 us (6%)
  starting transfers between devices  42 us (6%)
  local copies, waits for them, and re-layouts  38.1 us (5%)
  other arithmetic  17.5 us (2%)
  between operations  14.6 us (2%)
  Pallas kernels  13.1 us (2%)
    all_to_all x4, waiting for transfers between devices, dispatch(): return lax.all_to_all(rows, ('y', 'x'), 0, 0, tiled=True)  243 us
    all_gather x2, waiting for transfers between devices, gather_grad(): full = lax.all_gather(grad, ('y', 'z'), axis=0, tiled=True)  154 us
    ppermute x2, waiting for transfers between devices, to_owner_core(): return lax.ppermute(grad, ('y', 'c'), pairs)  36 us
    all_gather x1, blocking collectives, small_psum(): lax.all_gather(part, ('z', 'y'), axis=0, tiled=False)  25.9 us
    all_to_all x4, starting transfers between devices, dispatch(): return lax.all_to_all(rows, ('y', 'x'), 0, 0, tiled=True)  22.2 us
    transpose x1, local copies, waits for them, and re-layouts, local_step(): full_up = jnp.swapaxes(gate_up[:, ff:], 1, 2)  18.7 us
    dot_general x2, matrix products, reduce_grad(): jnp.einsum('rf,rm->fm', here, rows, preferred_element_type=F32) + sent  17.7 us
    all_gather x1, blocking collectives, small_psum(): full = lax.all_gather(part, ('x', 'c'), axis=0, tiled=False)  17.1 us
  transfers between devices with their start and end apart: 16, of which 8 were waited for; matrix products, arithmetic and copies ran while one was open for 17% of the time, Pallas kernels for 2%

profile of v1, /device:TPU:1, one launch (start us, length us, event | category | flops | bytes accessed | tf_op | source)
XLA Modules:
  0.0 710.4 jit_solution(15006340823000428303)
XLA Ops:
  7.2 2.1 convert_reduce_fusion.1
  9.4 2.3 fusion.16
  11.7 0.2 fusion.40
  12.0 1.0 fusion.11
  13.0 3.9 convolution_convert_fusion.1
  16.9 7.6 %all-to-all-start = ((bf16[16,40,4096]{2,1,0:T(8,128)(2,1)}), bf16[16,40,4096]{2,1,0:T(8,128)(2,1)}, u32[]{:S(2)}, u32[]{:S(2)}) async-start(bf16[16,40,4096]{2,1,0:T(8,128)(2,1)} %bitcast.66), calls=%async_computation | async-start | bytes 10485760 | tf_op jit(solution)/shard_map/all_to_all | solution.py:75
  24.6 4.3 dynamic-slice_bitcast_fusion.2
  28.8 1.4 collective-permute-start
  30.2 4.3 dynamic-slice_bitcast_fusion.1
  34.5 1.4 collective-permute-start.1
  36.0 2.5 convert_element_type.79
  38.4 0.6 fusion.66
  39.2 6.5 bitcast_convert_fusion
  45.7 56.3 %all-to-all-done = bf16[16,40,4096]{2,1,0:T(8,128)(2,1)} async-done(((bf16[16,40,4096]{2,1,0:T(8,128)(2,1)}), bf16[16,40,4096]{2,1,0:T(8,128)(2,1)}, u32[]{:S(2)}, u32[]{:S(2)}) %all-to-all-start) | async-done | bytes 5242912 | tf_op jit(solution)/shard_map/all_to_all | solution.py:75
  102.0 5.1 all-to-all-start.1
  107.1 0.0 reduce-scatter.3.cloned.1.call-start
  107.1 4.3 dynamic-slice_bitcast_fusion
  111.4 1.8 collective-permute-start.2
  113.3 6.7 fusion.28
  120.0 7.8 %fusion.30 = (bf16[640,448]{0,1:T(8,128)(2,1)S(1)}, bf16[640,448]{0,1:T(8,128)(2,1)}) fusion(bf16[640,448]{0,1:T(8,128)(2,1)S(1)} %fusion.28, bf16[640,4096]{1,0:T(8,128)(2,1)} %bitcast.1, bf16[4096,448]{0,1:T(8,128)(2,1)} %dynamic-slice_bitcast_fusion.1, bf16[4096,448]{0,1:T(8,128)(2,1)} %collective-permute-done.1, pred[]{:T(512)S(6)} %eq.47), kind=kOutput, calls=%fused_computation.61 | convolution fusion | flops 2353225728 | bytes 14303233 | tf_op jit(solution)/shard_map/dot_general | solution.py:151
  127.8 7.3 %convolution_convert_fusion = bf16[640,4096]{1,0:T(8,128)(2,1)} fusion(bf16[640,448]{0,1:T(8,128)(2,1)S(1)} %get-tuple-element.36, bf16[448,4096]{1,0:T(8,128)(2,1)} %dynamic-slice_bitcast_fusion, bf16[448,4096]{1,0:T(8,128)(2,1)} %collective-permute-done.2, pred[]{:T(512)S(6)} %eq.47), kind=kOutput, calls=%fused_computation.7 | convolution fusion | flops 2353266688 | bytes 13156353 | tf_op jit(solution)/shard_map/dot_general | solution.py:156
  135.1 47.1 %all-to-all-done.1 = bf16[16,40,4096]{2,1,0:T(8,128)(2,1)} async-done(((bf16[16,40,4096]{2,1,0:T(8,128)(2,1)}), bf16[16,40,4096]{2,1,0:T(8,128)(2,1)}, u32[]{:S(2)}, u32[]{:S(2)}) %all-to-all-start.1) | async-done | bytes 5242912 | tf_op jit(solution)/shard_map/all_to_all | solution.py:75
  182.2 4.2 fusion.48
  186.4 3.1 collective-permute-start.3
  189.5 7.0 fusion.33
  196.5 7.9 %fusion.43 = f32[448,4096]{1,0:T(8,128)} fusion(bf16[640,4096]{1,0:T(8,128)(2,1)} %bitcast.1, bf16[640,448]{0,1:T(8,128)(2,1)S(1)} %get-tuple-element.38, pred[]{:T(512)S(6)} %eq.48, bf16[640,448]{0,1:T(8,128)(2,1)S(1)} %copy-done.7, bf16[640,448]{0,1:T(8,128)(2,1)S(1)} %get-tuple-element.39), kind=kOutput, calls=%fused_computation.74 | convolution fusion | flops 2351390720 | bytes 14303233 | tf_op jit(solution)/shard_map/rf,rm->fm/dot_general | solution.py:83
  204.4 0.0 collective-permute-start.5
  204.4 6.0 convolution_add_fusion.2
  210.4 0.0 reduce-scatter.5.cloned.1.call-start
  210.5 5.9 collective-permute-done.5
  216.4 11.7 %convolution_add_fusion = f32[448,4096]{1,0:T(8,128)} fusion(f32[448,4096]{1,0:T(8,128)} %collective-permute-done.5, bf16[640,4096]{1,0:T(8,128)(2,1)} %bitcast.1, bf16[640,448]{0,1:T(8,128)(2,1)S(1)} %get-tuple-element.38, pred[]{:T(512)S(6)} %eq.48, bf16[640,448]{0,1:T(8,128)(2,1)S(1)} %copy-done.8, bf16[640,448]{0,1:T(8,128)(2,1)} %copy-done.9), kind=kOutput, calls=%fused_computation.15 | convolution fusion | flops 2353225728 | bytes 21643264 | tf_op jit(solution)/shard_map/rf,rm->fm/dot_general | solution.py:85
  228.1 4.8 all-to-all-start.2
  233.0 5.1 fusion.23
  238.1 7.8 %add_convert_fusion = bf16[640,4096]{1,0:T(8,128)(2,1)} fusion(f32[640,4096]{1,0:T(8,128)S(1)} %fusion.23, bf16[640,448]{0,1:T(8,128)(2,1)S(1)} %get-tuple-element.38, bf16[4096,448]{0,1:T(8,128)(2,1)} %dynamic-slice_bitcast_fusion.2, bf16[4096,448]{0,1:T(8,128)(2,1)} %collective-permute-done, pred[]{:T(512)S(6)} %eq.47), kind=kOutput, calls=%fused_computation.3 | convolution fusion | flops 2355888128 | bytes 23642112 | tf_op jit(solution)/shard_map/rf,mf->rm/dot_general | solution.py:167
  245.8 66.8 %all-to-all-done.2 = bf16[16,40,4096]{2,1,0:T(8,128)(2,1)} async-done(((bf16[16,40,4096]{2,1,0:T(8,128)(2,1)}), bf16[16,40,4096]{2,1,0:T(8,128)(2,1)}, u32[]{:S(2)}, u32[]{:S(2)}) %all-to-all-start.2) | async-done | bytes 5242912 | tf_op jit(solution)/shard_map/all_to_all | solution.py:75
  312.6 4.7 all-to-all-start.3
  317.4 0.0 all-gather.9.cloned.1.call-start
  317.4 0.0 reduce-scatter.3.cloned.1.call-done
  317.5 4.3 collective-permute-start.4
  321.7 73.0 %all-to-all-done.3 = bf16[16,40,4096]{2,1,0:T(8,128)(2,1)} async-done(((bf16[16,40,4096]{2,1,0:T(8,128)(2,1)}), bf16[16,40,4096]{2,1,0:T(8,128)(2,1)}, u32[]{:S(2)}, u32[]{:S(2)}) %all-to-all-start.3) | async-done | bytes 5242912 | tf_op jit(solution)/shard_map/all_to_all | solution.py:75
  394.7 0.9 copy-done.12
  395.6 0.0 all-gather.9.cloned.1.call-update
  395.7 0.0 all-gather.7.cloned.1.call-start
  395.7 3.9 collective-permute-start.6
  399.6 36.0 %collective-permute-done.6 = f32[112,4096]{1,0:T(8,128)} collective-permute-done((f32[112,4096]{1,0:T(8,128)}, f32[112,4096]{1,0:T(8,128)}, u32[]{:S(2)}, u32[]{:S(2)}) %collective-permute-start.6) | collective-permute-done | bytes 1835040 | tf_op jit(solution)/shard_map/ppermute | solution.py:71
  435.5 0.0 all-gather.7.cloned.1.call-update
  435.6 2.3 fusion.86
  438.0 4.1 copy.38
  442.1 10.5 %multiply_reduce_fusion = (f32[256,2]{0,1:T(2,128)S(1)}, f32[256,4096]{1,0:T(8,128)}) fusion(f32[256,4096]{1,0:T(8,128)} %convert_element_type.79, f32[256,2]{0,1:T(2,128)S(1)} %copy-done.34, bf16[640,4096]{1,0:T(8,128)(2,1)} %bitcast.9, s32[256,2]{0,1:T(2,128)S(1)} %copy-done.31), kind=kOutput, calls=%fused_computation.4 | convolution fusion | flops 2692021760 | bytes 13637632 | tf_op jit(solution)/shard_map/dot_general | solution.py:177
  452.7 0.6 fusion.57
  453.3 0.7 fusion.67
  454.1 7.4 %fusion.19 = (f32[4096]{0:T(1024)S(1)}, f32[256]{0:T(256)S(1)}, f32[256]{0:T(256)S(1)}, f32[4096]{0:T(1024)S(1)}, bf16[256,4096]{1,0:T(8,128)(2,1)}) fusion(bf16[256,4096]{1,0:T(8,128)(2,1)S(1)} %copy-done.1, f32[256]{0:T(256)S(1)} %copy-done.28, f32[256]{0:T(256)S(1)} %copy-done.21, f32[4096]{0:T(1024)S(1)} %copy-done.13, f32[256,4096]{1,0:T(8,128)S(1)} %fusion.67, ...), kind=kOutput, calls=%fused_computation.37 | convolution fusion | flops 1355800064 | bytes 14012416 | tf_op jit(solution)/shard_map/ts,sm->tm/dot_general | solution.py:181
  461.5 0.8 maximum_bitcast_fusion
  462.3 3.7 all-to-all-start.4
  466.0 6.1 fusion.15
  472.0 1.3 all-to-all-done.4
  473.4 25.9 %all-gather.2 = f32[16,18,512]{2,1,0:T(8,128)S(1)} all-gather(f32[1,18,512]{2,1,0:T(8,128)S(1)} %bitcast.76), channel_id=2, replica_groups=mesh['z'=4,'y'=4,'x'=4,'c'=2] {'z','y'}, dimensions={0}, use_global_device_ids=true | all-gather | bytes 626688 | tf_op jit(solution)/shard_map/all_gather | solution.py:118
  499.3 0.1 reduce_sum.152
  499.3 17.1 %all-gather.3 = f32[8,18,512]{2,1,0:T(8,128)S(1)} all-gather(f32[1,18,512]{2,1,0:T(8,128)S(1)} %bitcast.75), channel_id=3, replica_groups=mesh['z'=4,'y'=4,'x'=4,'c'=2] {'x','c'}, dimensions={0}, use_global_device_ids=true | all-gather | bytes 331776 | tf_op jit(solution)/shard_map/all_gather | solution.py:119
  516.5 0.7 copy.39
  517.2 0.6 fusion.65
  517.8 13.1 %shard_map.161 = f32[2,448,4096]{2,1,0:T(8,128)} custom-call(f32[2,448,4096]{2,1,0:T(8,128)} %bitcast.69), custom_call_target="tpu_custom_call" | custom-call | flops 5000000000 | bytes 29360128 | tf_op jit(solution)/shard_map/pallas_call | solution.py:96
  530.9 153.9 %all-gather.7.cloned.1.call-done = f32[1792,4096]{1,0:T(8,128)} async-done(((f32[112,4096]{1,0:T(8,128)}), f32[1792,4096]{1,0:T(8,128)}) %all-gather.7.cloned.1.call-update) | async-done | bytes 29360144 | tf_op jit(solution)/shard_map/all_gather | solution.py:107
  684.9 18.7 %slice_bitcast_fusion = (f32[2,4096,448]{1,2,0:T(8,128)}, f32[2,4096,448]{1,2,0:T(8,128)}) fusion(f32[2,896,4096]{2,1,0:T(8,128)} %bitcast.65), kind=kLoop, calls=%fused_computation | loop fusion | bytes 58720256 | tf_op jit(solution)/shard_map/transpose | solution.py:175
  (93 shorter events, 0.4 us)
Async XLA Ops:
  7.2 31.3 %copy-start = (bf16[4096,16]{0,1:T(8,128)(2,1)S(1)}, bf16[4096,16]{0,1:T(8,128)(2,1)}, u32[]{:S(2)}) copy-start(bf16[4096,16]{0,1:T(8,128)(2,1)} %param.13) | copy-start | bytes 393220
  7.2 4.7 copy-start.1
  7.2 4.5 copy-start.32
  7.2 4.5 copy-start.23
  7.2 4.7 copy-start.13
  7.2 4.7 copy-start.16
  9.3 2.6 copy-start.20
  11.7 5.2 copy-start.27
  11.7 27.5 %copy-start.30 = (s32[256,2]{0,1:T(2,128)}, s32[256,2]{0,1:T(2,128)S(1)}, u32[]{:S(2)}) copy-start(s32[256,2]{0,1:T(2,128)S(1)} %compare_select_fusion) | copy-start | bytes 6148
  12.0 5.0 copy-start.10
  13.0 3.9 copy-start.2
  16.9 85.1 %all-to-all-start = ((bf16[16,40,4096]{2,1,0:T(8,128)(2,1)}), bf16[16,40,4096]{2,1,0:T(8,128)(2,1)}, u32[]{:S(2)}, u32[]{:S(2)}) async-start(bf16[16,40,4096]{2,1,0:T(8,128)(2,1)} %bitcast.66), calls=%async_computation | async-start | bytes 10485760 | tf_op jit(solution)/shard_map/all_to_all | solution.py:75
  28.8 7.1 %copy-start.4 = (bf16[256,4096]{1,0:T(8,128)(2,1)S(1)}, bf16[256,4096]{1,0:T(8,128)(2,1)}, u32[]{:S(2)}) copy-start(bf16[256,4096]{1,0:T(8,128)(2,1)} %param.19) | copy-start | bytes 6291460
  28.8 84.4 %collective-permute-start = (bf16[4096,448]{0,1:T(8,128)(2,1)}, bf16[4096,448]{0,1:T(8,128)(2,1)}, u32[]{:S(2)}, u32[]{:S(2)}) collective-permute-start(bf16[4096,448]{0,1:T(8,128)(2,1)} %dynamic-slice_bitcast_fusion.2), channel_id=1, source_target_pairs={{0,1},{9,8},{16,17},{25,24},{2,3},{11,10},{18,19},{27,26},{4,5},{1... | collective-permute-start | bytes 11010056 | tf_op jit(solution)/shard_map/ppermute | solution.py:61
  34.5 3.9 copy-start.3
  34.5 85.5 %collective-permute-start.1 = (bf16[4096,448]{0,1:T(8,128)(2,1)}, bf16[4096,448]{0,1:T(8,128)(2,1)}, u32[]{:S(2)}, u32[]{:S(2)}) collective-permute-start(bf16[4096,448]{0,1:T(8,128)(2,1)} %dynamic-slice_bitcast_fusion.1), channel_id=1, source_target_pairs={{0,1},{9,8},{16,17},{25,24},{2,3},{11,10},{18,19},{27,26},{4,5},{1... | collective-permute-start | bytes 11010056 | tf_op jit(solution)/shard_map/ppermute | solution.py:61
  39.1 6.6 copy-start.14
  39.2 6.5 copy-start.18
  39.2 6.5 copy-start.25
  39.2 6.5 copy-start.33
  102.0 80.2 %all-to-all-start.1 = ((bf16[16,40,4096]{2,1,0:T(8,128)(2,1)}), bf16[16,40,4096]{2,1,0:T(8,128)(2,1)}, u32[]{:S(2)}, u32[]{:S(2)}) async-start(bf16[16,40,4096]{2,1,0:T(8,128)(2,1)} %bitcast.71), calls=%async_computation.1 | async-start | bytes 10485760 | tf_op jit(solution)/shard_map/all_to_all | solution.py:75
  107.1 210.4 %reduce-scatter.3.cloned.1.call-start = ((), (), s32[]{:S(2)}) async-start(), calls=%async_computation.7 | async-start | bytes 4587520 | tf_op jit(solution)/shard_map/reduce_scatter | solution.py:86
  111.4 16.3 %collective-permute-start.2 = (bf16[448,4096]{1,0:T(8,128)(2,1)}, bf16[448,4096]{1,0:T(8,128)(2,1)}, u32[]{:S(2)}, u32[]{:S(2)}) collective-permute-start(bf16[448,4096]{1,0:T(8,128)(2,1)} %dynamic-slice_bitcast_fusion), channel_id=1, source_target_pairs={{0,1},{9,8},{16,17},{25,24},{2,3},{11,10},{18,19},{27,26},{4,5},{1... | collective-permute-start | bytes 11010056 | tf_op jit(solution)/shard_map/ppermute | solution.py:61
  120.0 7.8 %copy-start.6 = (bf16[640,448]{0,1:T(8,128)(2,1)}, bf16[640,448]{0,1:T(8,128)(2,1)S(1)}, u32[]{:S(2)}) copy-start(bf16[640,448]{0,1:T(8,128)(2,1)S(1)} %fusion.28) | copy-start | bytes 1720324
  182.2 7.3 %copy-start.7 = (bf16[640,448]{0,1:T(8,128)(2,1)S(1)}, bf16[640,448]{0,1:T(8,128)(2,1)}, u32[]{:S(2)}) copy-start(bf16[640,448]{0,1:T(8,128)(2,1)} %copy-done.6) | copy-start | bytes 1720324
  182.2 7.3 %copy-start.35 = (bf16[640,448]{0,1:T(8,128)(2,1)S(1)}, bf16[640,448]{0,1:T(8,128)(2,1)}, u32[]{:S(2)}) copy-start(bf16[640,448]{0,1:T(8,128)(2,1)} %get-tuple-element.37) | copy-start | bytes 1720324
  186.4 18.0 %collective-permute-start.3 = (f32[224,4096]{1,0:T(8,128)S(1)}, f32[224,4096]{1,0:T(8,128)S(1)}, u32[]{:S(2)}, u32[]{:S(2)}) collective-permute-start(f32[224,4096]{1,0:T(8,128)S(1)} %fusion.48), channel_id=1, source_target_pairs={{0,1},{1,0},{2,3},{3,2},{4,5},{5,4},{6,7},{7,6},{8,9},{9,8},{10,11... | collective-permute-start | bytes 11010056 | tf_op jit(solution)/shard_map/ppermute | solution.py:84
  196.5 7.9 %copy-start.9 = (bf16[640,448]{0,1:T(8,128)(2,1)}, bf16[640,448]{0,1:T(8,128)(2,1)S(1)}, u32[]{:S(2)}) copy-start(bf16[640,448]{0,1:T(8,128)(2,1)S(1)} %get-tuple-element.39) | copy-start | bytes 1720324
  204.4 12.0 %collective-permute-start.5 = (f32[448,4096]{1,0:T(8,128)}, f32[448,4096]{1,0:T(8,128)}, u32[]{:S(2)}, u32[]{:S(2)}) collective-permute-start(f32[448,4096]{1,0:T(8,128)} %fusion.43), channel_id=1, source_target_pairs={{0,1},{1,0},{2,3},{3,2},{4,5},{5,4},{6,7},{7,6},{8,9},{9,8},{10,11... | collective-permute-start | bytes 22020104 | tf_op jit(solution)/shard_map/ppermute | solution.py:84
  210.4 6.0 copy-start.8
  210.4 184.3 %reduce-scatter.5.cloned.1.call-start = ((), (), s32[]{:S(2)}) async-start(), calls=%async_computation.8 | async-start | bytes 9175040 | tf_op jit(solution)/shard_map/reduce_scatter | solution.py:86
  228.1 84.5 %all-to-all-start.2 = ((bf16[16,40,4096]{2,1,0:T(8,128)(2,1)}), bf16[16,40,4096]{2,1,0:T(8,128)(2,1)}, u32[]{:S(2)}, u32[]{:S(2)}) async-start(bf16[16,40,4096]{2,1,0:T(8,128)(2,1)} %bitcast.68), calls=%async_computation.2 | async-start | bytes 10485760 | tf_op jit(solution)/shard_map/all_to_all | solution.py:75
  312.6 122.9 %copy-start.17 = (f32[4096]{0:T(1024)S(1)}, f32[4096]{0:T(1024)}, u32[]{:S(2)}) copy-start(f32[4096]{0:T(1024)} %param.12) | copy-start | bytes 49156
  312.6 122.9 %copy-start.21 = (f32[256]{0:T(256)S(1)}, f32[256]{0:T(256)}, u32[]{:S(2)}) copy-start(f32[256]{0:T(256)} %copy-done.20) | copy-start | bytes 3076
  312.6 122.9 %copy-start.28 = (f32[256]{0:T(256)S(1)}, f32[256]{0:T(256)}, u32[]{:S(2)}) copy-start(f32[256]{0:T(256)} %copy-done.27) | copy-start | bytes 3076
  312.6 82.1 %all-to-all-start.3 = ((bf16[16,40,4096]{2,1,0:T(8,128)(2,1)}), bf16[16,40,4096]{2,1,0:T(8,128)(2,1)}, u32[]{:S(2)}, u32[]{:S(2)}) async-start(bf16[16,40,4096]{2,1,0:T(8,128)(2,1)} %bitcast.67), calls=%async_computation.5 | async-start | bytes 10485760 | tf_op jit(solution)/shard_map/all_to_all | solution.py:75
  317.4 200.4 %all-gather.9.cloned.1.call-start = ((), (), s32[]{:S(2)}) async-start(), calls=%async_computation.10 | async-start | bytes 15597568 | tf_op jit(solution)/shard_map/all_gather | solution.py:107
  317.5 77.3 %collective-permute-start.4 = (f32[56,4096]{1,0:T(8,128)}, f32[56,4096]{1,0:T(8,128)S(1)}, u32[]{:S(2)}, u32[]{:S(2)}) collective-permute-start(f32[56,4096]{1,0:T(8,128)} %reduce-scatter.3.cloned.1.call-done), channel_id=1, source_target_pairs={{0,0},{1,8},{9,9},{8,1},{16,16},{17,24},{25,25},{24,17},{2,2},{3,1... | collective-permute-start | bytes 2752520 | tf_op jit(solution)/shard_map/ppermute | solution.py:71
  394.7 0.9 copy-start.12
  395.7 289.2 %all-gather.7.cloned.1.call-start = ((), (), s32[]{:S(2)}) async-start(), calls=%async_computation.9 | async-start | bytes 31195136 | tf_op jit(solution)/shard_map/all_gather | solution.py:107
  395.7 39.8 %collective-permute-start.6 = (f32[112,4096]{1,0:T(8,128)}, f32[112,4096]{1,0:T(8,128)}, u32[]{:S(2)}, u32[]{:S(2)}) collective-permute-start(f32[112,4096]{1,0:T(8,128)} %reduce-scatter.5.cloned.1.call-done), channel_id=1, source_target_pairs={{0,0},{1,8},{9,9},{8,1},{16,16},{17,24},{25,25},{24,17},{2,2},{3,1... | collective-permute-start | bytes 5505032 | tf_op jit(solution)/shard_map/ppermute | solution.py:71
  435.6 6.4 copy-start.31
  435.6 6.4 copy-start.34
  442.0 10.5 %copy-start.15 = (f32[256,2]{0,1:T(2,128)S(1)}, f32[256,2]{0,1:T(2,128)}, u32[]{:S(2)}) copy-start(f32[256,2]{0,1:T(2,128)} %copy-done.14) | copy-start | bytes 6148
  442.0 10.5 %copy-start.19 = (f32[256]{0:T(256)S(1)}, f32[256]{0:T(256)}, u32[]{:S(2)}) copy-start(f32[256]{0:T(256)} %copy-done.18) | copy-start | bytes 3076
  442.0 10.5 %copy-start.26 = (f32[256]{0:T(256)S(1)}, f32[256]{0:T(256)}, u32[]{:S(2)}) copy-start(f32[256]{0:T(256)} %copy-done.25) | copy-start | bytes 3076
  442.1 10.6 %copy-start.24 = (s32[256,2]{0,1:T(2,128)S(1)}, s32[256,2]{0,1:T(2,128)}, u32[]{:S(2)}) copy-start(s32[256,2]{0,1:T(2,128)} %param.17) | copy-start | bytes 6148
  442.1 10.6 %copy-start.5 = (bf16[4096,256]{1,0:T(8,128)(2,1)S(1)}, bf16[4096,256]{1,0:T(8,128)(2,1)}, u32[]{:S(2)}) copy-start(bf16[4096,256]{1,0:T(8,128)(2,1)} %copy.38) | copy-start | bytes 6291460
  452.6 1.5 copy-start.11
  454.1 11.9 %copy-start.22 = (f32[256]{0:T(256)S(1)}, f32[256]{0:T(256)}, u32[]{:S(2)}) copy-start(f32[256]{0:T(256)} %copy-done.20) | copy-start | bytes 3076
  454.1 11.9 %copy-start.29 = (f32[256]{0:T(256)S(1)}, f32[256]{0:T(256)}, u32[]{:S(2)}) copy-start(f32[256]{0:T(256)} %copy-done.27) | copy-start | bytes 3076
  462.3 11.1 %all-to-all-start.4 = ((f32[8,18,512]{2,1,0:T(8,128)}), f32[8,18,512]{2,1,0:T(8,128)S(1)}, u32[]{:S(2)}, u32[]{:S(2)}) async-start(f32[8,18,512]{2,1,0:T(8,128)} %maximum_bitcast_fusion), calls=%async_computation.6 | async-start | bytes 786432 | tf_op jit(solution)/shard_map/all_to_all | solution.py:116
Sparse Core Ops, SparseCore 0:
  210.5 42.9 reduce-scatter.2
  256.5 72.3 reduce-scatter.4
  395.8 111.6 all-gather.8
  509.6 175.2 all-gather.6
